TPU v7x, 32 devices: a whole 2x2x4 slice. The times are simulated.
32 devices in a mesh: data: 32 (over z, y, x, core).
Axes of the slice: x: 2, y: 2, z: 4, core: 2. Of those that a mesh axis runs over, the one named last changes fastest.
Arguments:
- w_one: float32 [8, 768, 2048], P(None, 'data')
- w_two: float32 [8, 2048, 768], P(None, 'data')
- mom_one: float32 [8, 768, 2048], P(None, 'data')
- mom_two: float32 [8, 2048, 768], P(None, 'data')
- x_zero: bfloat16 [32768, 768], P('data')
- y_zero: bfloat16 [32768, 768], P('data')
- x_one: bfloat16 [32768, 768], P('data')
- y_one: bfloat16 [32768, 768], P('data')
Outputs:
- output 1: float32 [8, 768, 2048], P(None, 'data')
- output 2: float32 [8, 2048, 768], P(None, 'data')
- output 3: float32 [8, 768, 2048], P(None, 'data')
- output 4: float32 [8, 2048, 768], P(None, 'data')
- output 5: float32 [32768], P('data')
- output 6: float32 [32768, 768], P('data')
All inputs are finite; a program needn't handle non-finite values.
Results may differ from a plain program's by a relative error of at most 0.0089424.
Values are sent between devices in bfloat16 or wider.
A program may use at most 1 GiB of HBM per device.

v0:
```python
import jax
import jax.numpy as jnp
from jax import lax
from jax.sharding import PartitionSpec as P

LEARN_RATE = 0.1
MOMENTUM = 0.9


def run_stack(w_one_b, w_two_b, h_cur):
    saved_vals = []
    for layer_idx in range(w_one_b.shape[0]):
        act_in = h_cur.astype(jnp.bfloat16)
        pre_act = jnp.dot(act_in, w_one_b[layer_idx], preferred_element_type=jnp.float32)
        hidden, gelu_back = jax.vjp(jax.nn.gelu, pre_act)
        hidden = hidden.astype(jnp.bfloat16)
        h_cur = h_cur + jnp.dot(hidden, w_two_b[layer_idx], preferred_element_type=jnp.float32)
        saved_vals.append((act_in, hidden, gelu_back))
    return h_cur, saved_vals


def layer_grads(d_state, w_out, layer_vals):
    act_in, hidden, gelu_back = layer_vals
    d_low = d_state.astype(jnp.bfloat16)
    grad_out = jnp.einsum("tf,td->fd", hidden, d_low, preferred_element_type=jnp.float32).astype(jnp.bfloat16)
    d_hidden = jnp.einsum("td,fd->tf", d_low, w_out, preferred_element_type=jnp.float32)
    d_pre = gelu_back(d_hidden)[0].astype(jnp.bfloat16)
    grad_in = jnp.einsum("td,tf->df", act_in, d_pre, preferred_element_type=jnp.float32).astype(jnp.bfloat16)
    return grad_in, grad_out, d_pre


def solution(mesh):
    n_dev = mesh.shape["data"]
    w_spec = P(None, "data", None)
    row_spec = P("data", None)

    def device_step(w_one, w_two, mom_one, mom_two, x_zero, y_zero, x_one, y_one):
        layers = w_one.shape[0]
        tok_dev, d_model = x_zero.shape
        w_one_b = lax.all_gather(w_one.astype(jnp.bfloat16), "data", axis=1, tiled=True)
        w_two_b = lax.all_gather(w_two.astype(jnp.bfloat16), "data", axis=1, tiled=True)
        h_end, saved_vals = run_stack(w_one_b, w_two_b, x_zero.astype(jnp.float32))
        d_state = (h_end - y_zero.astype(jnp.float32)) / (n_dev * tok_dev * d_model)
        shard_in = [None] * layers
        shard_out = [None] * layers
        for layer_idx in reversed(range(layers)):
            grad_in, grad_out, d_pre = layer_grads(d_state, w_two_b[layer_idx], saved_vals[layer_idx])
            shard_out[layer_idx] = lax.psum_scatter(grad_out, "data", scatter_dimension=0, tiled=True)
            shard_in[layer_idx] = lax.psum_scatter(grad_in, "data", scatter_dimension=0, tiled=True)
            if layer_idx > 0:
                d_state = d_state + jnp.einsum("tf,df->td", d_pre, w_one_b[layer_idx], preferred_element_type=jnp.float32)
        new_mom_one = MOMENTUM * mom_one + jnp.stack(shard_in).astype(jnp.float32)
        new_mom_two = MOMENTUM * mom_two + jnp.stack(shard_out).astype(jnp.float32)
        new_w_one = w_one - LEARN_RATE * new_mom_one
        new_w_two = w_two - LEARN_RATE * new_mom_two
        next_one_b = lax.all_gather(new_w_one.astype(jnp.bfloat16), "data", axis=1, tiled=True)
        next_two_b = lax.all_gather(new_w_two.astype(jnp.bfloat16), "data", axis=1, tiled=True)
        h_last = run_stack(next_one_b, next_two_b, x_one.astype(jnp.float32))[0]
        loss_rows = jnp.sum(jnp.square(h_last - y_one.astype(jnp.float32)), axis=1) / (2 * d_model)
        return new_w_one, new_w_two, new_mom_one, new_mom_two, loss_rows, h_last

    return jax.shard_map(device_step, mesh=mesh, in_specs=(w_spec, w_spec, w_spec, w_spec, row_spec, row_spec, row_spec, row_spec), out_specs=(w_spec, w_spec, w_spec, w_spec, P("data"), row_spec), check_vma=False)
```

profile of v0, /device:TPU:17, one launch (start us, length us, event | category | flops | bytes accessed | tf_op | source)
XLA Modules:
  0.0 2744.5 jit_solution(3491272767817243826)
XLA Ops:
  12.1 153.3 %all-gather.5.cloned.1.call-done = bf16[8,768,2048]{2,1,0:T(8,128)(2,1)} async-done(((bf16[8,24,2048]{2,1,0:T(8,128)(2,1)}), bf16[8,768,2048]{2,1,0:T(8,128)(2,1)}) %all-gather.5.cloned.1.call-update) | async-done | bytes 25165840 | tf_op jit(solution)/shard_map/all_gather | solution.py:40
  165.4 9.0 fusion.140
  174.5 146.5 %all-gather.7.cloned.1.call-done = bf16[8,2048,768]{2,1,0:T(8,128)(2,1)} async-done(((bf16[8,64,768]{2,1,0:T(8,128)(2,1)}), bf16[8,2048,768]{2,1,0:T(8,128)(2,1)}) %all-gather.7.cloned.1.call-update) | async-done | bytes 25165840 | tf_op jit(solution)/shard_map/all_gather | solution.py:41
  335.9 9.3 fusion.181
  354.9 10.3 fusion.194
  427.3 11.0 subtract_multiply_fusion
  438.3 12.9 fusion.55
  458.6 14.5 fusion.48
  480.4 14.6 fusion.41
  502.4 14.4 fusion.34
  524.0 14.4 fusion.27
  545.8 14.6 fusion.20
  567.8 13.0 fusion.13
  589.4 14.7 fusion.148
  663.2 10.4 convolution_convert_fusion.7
  673.7 11.0 convolution_convert_fusion.6
  685.2 10.0 convolution_convert_fusion.5
  695.3 11.1 convolution_convert_fusion.4
  706.6 10.1 convolution_convert_fusion.3
  716.8 11.0 convolution_convert_fusion.2
  728.3 10.0 convolution_convert_fusion.1
  738.4 11.0 convolution_convert_fusion
  751.1 61.0 %reduce-scatter.51.cloned.1.call-done = bf16[24,2048]{1,0:T(8,128)(2,1)} async-done(((bf16[768,2048]{1,0:T(8,128)(2,1)}), bf16[24,2048]{1,0:T(8,128)(2,1)}) %reduce-scatter.51.cloned.1.call-update) | async-done | bytes 98320 | tf_op jit(solution)/shard_map/reduce_scatter | solution.py:49
  813.6 104.9 %reduce-scatter.53.cloned.1.call-done = bf16[24,2048]{1,0:T(8,128)(2,1)} async-done(((bf16[768,2048]{1,0:T(8,128)(2,1)}), bf16[24,2048]{1,0:T(8,128)(2,1)}) %reduce-scatter.53.cloned.1.call-update) | async-done | bytes 98320 | tf_op jit(solution)/shard_map/reduce_scatter | solution.py:49
  920.1 105.5 %reduce-scatter.55.cloned.1.call-done = bf16[24,2048]{1,0:T(8,128)(2,1)} async-done(((bf16[768,2048]{1,0:T(8,128)(2,1)}), bf16[24,2048]{1,0:T(8,128)(2,1)}) %reduce-scatter.55.cloned.1.call-update) | async-done | bytes 98320 | tf_op jit(solution)/shard_map/reduce_scatter | solution.py:49
  1027.2 105.1 %reduce-scatter.57.cloned.1.call-done = bf16[24,2048]{1,0:T(8,128)(2,1)} async-done(((bf16[768,2048]{1,0:T(8,128)(2,1)}), bf16[24,2048]{1,0:T(8,128)(2,1)}) %reduce-scatter.57.cloned.1.call-update) | async-done | bytes 98320 | tf_op jit(solution)/shard_map/reduce_scatter | solution.py:49
  1133.8 105.2 %reduce-scatter.59.cloned.1.call-done = bf16[24,2048]{1,0:T(8,128)(2,1)} async-done(((bf16[768,2048]{1,0:T(8,128)(2,1)}), bf16[24,2048]{1,0:T(8,128)(2,1)}) %reduce-scatter.59.cloned.1.call-update) | async-done | bytes 98320 | tf_op jit(solution)/shard_map/reduce_scatter | solution.py:49
  1240.5 105.1 %reduce-scatter.61.cloned.1.call-done = bf16[24,2048]{1,0:T(8,128)(2,1)} async-done(((bf16[768,2048]{1,0:T(8,128)(2,1)}), bf16[24,2048]{1,0:T(8,128)(2,1)}) %reduce-scatter.61.cloned.1.call-update) | async-done | bytes 98320 | tf_op jit(solution)/shard_map/reduce_scatter | solution.py:49
  1347.2 105.0 %reduce-scatter.63.cloned.1.call-done = bf16[24,2048]{1,0:T(8,128)(2,1)} async-done(((bf16[768,2048]{1,0:T(8,128)(2,1)}), bf16[24,2048]{1,0:T(8,128)(2,1)}) %reduce-scatter.63.cloned.1.call-update) | async-done | bytes 98320 | tf_op jit(solution)/shard_map/reduce_scatter | solution.py:49
  1459.0 100.0 %reduce-scatter.33.cloned.1.call-done = bf16[64,768]{1,0:T(8,128)(2,1)} async-done(((bf16[2048,768]{1,0:T(8,128)(2,1)}), bf16[64,768]{1,0:T(8,128)(2,1)}) %reduce-scatter.33.cloned.1.call-update) | async-done | bytes 98320 | tf_op jit(solution)/shard_map/reduce_scatter | solution.py:48
  1560.5 104.9 %reduce-scatter.35.cloned.1.call-done = bf16[64,768]{1,0:T(8,128)(2,1)} async-done(((bf16[2048,768]{1,0:T(8,128)(2,1)}), bf16[64,768]{1,0:T(8,128)(2,1)}) %reduce-scatter.35.cloned.1.call-update) | async-done | bytes 98320 | tf_op jit(solution)/shard_map/reduce_scatter | solution.py:48
  1667.0 105.0 %reduce-scatter.37.cloned.1.call-done = bf16[64,768]{1,0:T(8,128)(2,1)} async-done(((bf16[2048,768]{1,0:T(8,128)(2,1)}), bf16[64,768]{1,0:T(8,128)(2,1)}) %reduce-scatter.37.cloned.1.call-update) | async-done | bytes 98320 | tf_op jit(solution)/shard_map/reduce_scatter | solution.py:48
  1773.6 104.9 %reduce-scatter.39.cloned.1.call-done = bf16[64,768]{1,0:T(8,128)(2,1)} async-done(((bf16[2048,768]{1,0:T(8,128)(2,1)}), bf16[64,768]{1,0:T(8,128)(2,1)}) %reduce-scatter.39.cloned.1.call-update) | async-done | bytes 98320 | tf_op jit(solution)/shard_map/reduce_scatter | solution.py:48
  1880.0 104.9 %reduce-scatter.41.cloned.1.call-done = bf16[64,768]{1,0:T(8,128)(2,1)} async-done(((bf16[2048,768]{1,0:T(8,128)(2,1)}), bf16[64,768]{1,0:T(8,128)(2,1)}) %reduce-scatter.41.cloned.1.call-update) | async-done | bytes 98320 | tf_op jit(solution)/shard_map/reduce_scatter | solution.py:48
  1986.5 104.9 %reduce-scatter.43.cloned.1.call-done = bf16[64,768]{1,0:T(8,128)(2,1)} async-done(((bf16[2048,768]{1,0:T(8,128)(2,1)}), bf16[64,768]{1,0:T(8,128)(2,1)}) %reduce-scatter.43.cloned.1.call-update) | async-done | bytes 98320 | tf_op jit(solution)/shard_map/reduce_scatter | solution.py:48
  2093.0 104.9 %reduce-scatter.45.cloned.1.call-done = bf16[64,768]{1,0:T(8,128)(2,1)} async-done(((bf16[2048,768]{1,0:T(8,128)(2,1)}), bf16[64,768]{1,0:T(8,128)(2,1)}) %reduce-scatter.45.cloned.1.call-update) | async-done | bytes 98320 | tf_op jit(solution)/shard_map/reduce_scatter | solution.py:48
  2199.4 104.9 %reduce-scatter.47.cloned.1.call-done = bf16[64,768]{1,0:T(8,128)(2,1)} async-done(((bf16[2048,768]{1,0:T(8,128)(2,1)}), bf16[64,768]{1,0:T(8,128)(2,1)}) %reduce-scatter.47.cloned.1.call-update) | async-done | bytes 98320 | tf_op jit(solution)/shard_map/reduce_scatter | solution.py:48
  2313.3 148.6 %all-gather.9.cloned.1.call-done = bf16[8,768,2048]{2,0,1:T(8,128)(2,1)} async-done(((bf16[8,24,2048]{2,0,1:T(8,128)(2,1)}), bf16[8,768,2048]{2,0,1:T(8,128)(2,1)}) %all-gather.9.cloned.1.call-update) | async-done | bytes 25165840 | tf_op jit(solution)/shard_map/all_gather | solution.py:56
  2461.9 107.9 %fusion.300 = (bf16[1,768,2048]{2,0,1:T(2,128)(2,1)}, bf16[1,768,2048]{2,0,1:T(2,128)(2,1)}, bf16[1,768,2048]{2,0,1:T(2,128)(2,1)}, bf16[1,768,2048]{2,0,1:T(2,1...) fusion(bf16[8,768,2048]{2,0,1:T(8,128)(2,1)} %all-gather.9.clon, ...), kind=kLoop, calls=%fused_computation.367 | loop fusion | bytes 50331648 | tf_op jit(solution)/shard_map/slice | solution.py:14
  2569.9 47.4 %all-gather.11.cloned.1.call-done = bf16[8,2048,768]{2,1,0:T(8,128)(2,1)} async-done(((bf16[8,64,768]{2,1,0:T(8,128)(2,1)}), bf16[8,2048,768]{2,1,0:T(8,128)(2,1)}) %all-gather.11.cloned.1.call-update) | async-done | bytes 25165840 | tf_op jit(solution)/shard_map/all_gather | solution.py:57
  2617.3 12.7 fusion.139
  2630.0 16.2 fusion.183
  2646.1 14.6 fusion.196
  2660.7 14.2 fusion.199
  2674.9 14.3 fusion.202
  2689.2 14.3 fusion.205
  2703.5 16.0 fusion.208
  2719.5 14.8 multiply_reduce_fusion
  (162 shorter events, 244.9 us)
Async XLA Ops:
  7.2 158.3 %all-gather.5.cloned.1.call-start = ((), (), s32[]{:S(2)}) async-start(), calls=%async_computation.16 | async-start | bytes 25952256 | tf_op jit(solution)/shard_map/all_gather | solution.py:40
  9.6 311.3 %all-gather.7.cloned.1.call-start = ((), (), s32[]{:S(2)}) async-start(), calls=%async_computation.17 | async-start | bytes 25952256 | tf_op jit(solution)/shard_map/all_gather | solution.py:41
  12.1 737.4 %reduce-scatter.49.cloned.1.call-start = ((), (), s32[]{:S(2)}) async-start(), calls=%async_computation.28 | async-start | bytes 3244032 | tf_op jit(solution)/shard_map/reduce_scatter | solution.py:49
  174.5 154.9 %copy-start.6 = (bf16[1024,768]{1,0:T(8,128)(2,1)S(1)}, bf16[1024,768]{1,0:T(8,128)(2,1)}, u32[]{:S(2)}) copy-start(bf16[1024,768]{1,0:T(8,128)(2,1)} %param.12) | copy-start | bytes 4718596
  329.4 6.5 copy-start.3
  335.9 9.3 copy-start.17
  346.9 18.3 slice-start
  346.9 18.3 slice-start.1
  346.9 18.3 slice-start.2
  354.8 10.4 slice-start.3
  354.8 10.4 slice-start.4
  354.9 10.4 slice-start.5
  393.2 6.1 copy-start.11
  421.6 5.7 copy-start.8
  438.3 12.9 copy-start.18
  458.6 14.5 copy-start.19
  480.4 14.6 copy-start.21
  502.4 14.4 copy-start.22
  524.0 14.4 copy-start.24
  545.8 14.6 copy-start.25
  567.8 15.1 copy-start.27
  607.0 205.1 %reduce-scatter.51.cloned.1.call-start = ((), (), s32[]{:S(2)}) async-start(), calls=%async_computation.29 | async-start | bytes 3244032 | tf_op jit(solution)/shard_map/reduce_scatter | solution.py:49
  615.8 8.5 copy-start.15
  615.9 302.7 %reduce-scatter.53.cloned.1.call-start = ((), (), s32[]{:S(2)}) async-start(), calls=%async_computation.30 | async-start | bytes 3244032 | tf_op jit(solution)/shard_map/reduce_scatter | solution.py:49
  624.3 401.4 %reduce-scatter.55.cloned.1.call-start = ((), (), s32[]{:S(2)}) async-start(), calls=%async_computation.31 | async-start | bytes 3244032 | tf_op jit(solution)/shard_map/reduce_scatter | solution.py:49
  631.6 8.5 copy-start.12
  631.6 500.6 %reduce-scatter.57.cloned.1.call-start = ((), (), s32[]{:S(2)}) async-start(), calls=%async_computation.32 | async-start | bytes 3244032 | tf_op jit(solution)/shard_map/reduce_scatter | solution.py:49
  640.1 598.9 %reduce-scatter.59.cloned.1.call-start = ((), (), s32[]{:S(2)}) async-start(), calls=%async_computation.33 | async-start | bytes 3244032 | tf_op jit(solution)/shard_map/reduce_scatter | solution.py:49
  647.3 8.6 copy-start.9
  647.3 698.4 %reduce-scatter.61.cloned.1.call-start = ((), (), s32[]{:S(2)}) async-start(), calls=%async_computation.34 | async-start | bytes 3244032 | tf_op jit(solution)/shard_map/reduce_scatter | solution.py:49
  655.8 796.5 %reduce-scatter.63.cloned.1.call-start = ((), (), s32[]{:S(2)}) async-start(), calls=%async_computation.35 | async-start | bytes 3244032 | tf_op jit(solution)/shard_map/reduce_scatter | solution.py:49
  663.0 896.0 %reduce-scatter.33.cloned.1.call-start = ((), (), s32[]{:S(2)}) async-start(), calls=%async_computation.18 | async-start | bytes 3244032 | tf_op jit(solution)/shard_map/reduce_scatter | solution.py:48
  673.7 11.6 copy-start.26
  673.7 991.8 %reduce-scatter.35.cloned.1.call-start = ((), (), s32[]{:S(2)}) async-start(), calls=%async_computation.19 | async-start | bytes 3244032 | tf_op jit(solution)/shard_map/reduce_scatter | solution.py:48
  684.8 1087.2 %reduce-scatter.37.cloned.1.call-start = ((), (), s32[]{:S(2)}) async-start(), calls=%async_computation.20 | async-start | bytes 3244032 | tf_op jit(solution)/shard_map/reduce_scatter | solution.py:48
  695.2 11.4 copy-start.23
  695.3 1183.2 %reduce-scatter.39.cloned.1.call-start = ((), (), s32[]{:S(2)}) async-start(), calls=%async_computation.21 | async-start | bytes 3244032 | tf_op jit(solution)/shard_map/reduce_scatter | solution.py:48
  706.4 1278.6 %reduce-scatter.41.cloned.1.call-start = ((), (), s32[]{:S(2)}) async-start(), calls=%async_computation.22 | async-start | bytes 3244032 | tf_op jit(solution)/shard_map/reduce_scatter | solution.py:48
  716.7 11.6 copy-start.20
  716.7 1374.7 %reduce-scatter.43.cloned.1.call-start = ((), (), s32[]{:S(2)}) async-start(), calls=%async_computation.23 | async-start | bytes 3244032 | tf_op jit(solution)/shard_map/reduce_scatter | solution.py:48
  727.8 1470.1 %reduce-scatter.45.cloned.1.call-start = ((), (), s32[]{:S(2)}) async-start(), calls=%async_computation.24 | async-start | bytes 3244032 | tf_op jit(solution)/shard_map/reduce_scatter | solution.py:48
  738.3 715.4 %copy-start = (f32[8,24,2048]{2,1,0:T(8,128)S(1)}, f32[8,24,2048]{2,1,0:T(8,128)}, u32[]{:S(2)}) copy-start(f32[8,24,2048]{2,1,0:T(8,128)} %param.8) | copy-start | bytes 4718596
  738.4 1566.0 %reduce-scatter.47.cloned.1.call-start = ((), (), s32[]{:S(2)}) async-start(), calls=%async_computation.25 | async-start | bytes 3244032 | tf_op jit(solution)/shard_map/reduce_scatter | solution.py:48
  749.4 1556.6 %copy-start.1 = (f32[8,64,768]{2,1,0:T(8,128)S(1)}, f32[8,64,768]{2,1,0:T(8,128)}, u32[]{:S(2)}) copy-start(f32[8,64,768]{2,1,0:T(8,128)} %param.9) | copy-start | bytes 4718596
  749.4 1712.5 %all-gather.9.cloned.1.call-start = ((), (), s32[]{:S(2)}) async-start(), calls=%async_computation.26 | async-start | bytes 25952256 | tf_op jit(solution)/shard_map/all_gather | solution.py:56
  1457.6 852.3 %copy-start.4 = (bf16[1024,768]{1,0:T(8,128)(2,1)S(1)}, bf16[1024,768]{1,0:T(8,128)(2,1)}, u32[]{:S(2)}) copy-start(bf16[1024,768]{1,0:T(8,128)(2,1)} %param.15) | copy-start | bytes 4718596
  1459.0 1158.3 %all-gather.11.cloned.1.call-start = ((), (), s32[]{:S(2)}) async-start(), calls=%async_computation.27 | async-start | bytes 25952256 | tf_op jit(solution)/shard_map/all_gather | solution.py:57
  2313.3 304.0 %copy-start.5 = (bf16[1024,768]{1,0:T(8,128)(2,1)S(1)}, bf16[1024,768]{1,0:T(8,128)(2,1)}, u32[]{:S(2)}) copy-start(bf16[1024,768]{1,0:T(8,128)(2,1)} %param.14) | copy-start | bytes 4718596
  (6 other events, 26.3 us)
Sparse Core Ops, SparseCore 0:
  11.4 154.0 all-gather.4
  168.8 152.0 all-gather.6
  607.1 98.4 reduce-scatter.48
  710.9 101.1 reduce-scatter.50
  817.4 101.1 reduce-scatter.52
  924.4 101.1 reduce-scatter.54
  1031.1 101.1 reduce-scatter.56
  1137.7 101.2 reduce-scatter.58
  1244.4 101.1 reduce-scatter.60
  1350.9 101.2 reduce-scatter.62
  1457.7 101.2 reduce-scatter.32
  1564.3 101.1 reduce-scatter.34
  1670.9 101.1 reduce-scatter.36
  1777.3 101.1 reduce-scatter.38
  1883.8 101.1 reduce-scatter.40
  1990.2 101.1 reduce-scatter.42
  2096.7 101.1 reduce-scatter.44
  2203.2 101.1 reduce-scatter.46
  2307.3 154.6 all-gather.8
  2465.2 152.0 all-gather.10
where the time goes:
time: 2750 us; the launch traced here: 2740 us
  waiting for transfers between devices  2020 us (73%)
  matrix products  545 us (20%)
  local copies, waits for them, and re-layouts  146 us (5%)
    reduce_scatter x8, waiting for transfers between devices, device_step(): lax.psum_scatter(grad_out, 'data', scatter_dimension=0, tiled=True)  835 us
    reduce_scatter x8, waiting for transfers between devices, device_step(): lax.psum_scatter(grad_in, 'data', scatter_dimension=0, tiled=True)  692 us
    dot_general x16, matrix products, run_stack(): jnp.dot(hidden, w_two_b[layer_idx], preferred_element_type=jnp.float32)  189 us
    all_gather x1, waiting for transfers between devices, device_step(): lax.all_gather(w_one.astype(jnp.bfloat16), 'data', axis=1, tiled=True)  153 us
    all_gather x1, waiting for transfers between devices, device_step(): lax.all_gather(new_w_one.astype(jnp.bfloat16), 'data', axis=1, tiled=True)  149 us
    all_gather x1, waiting for transfers between devices, device_step(): lax.all_gather(w_two.astype(jnp.bfloat16), 'data', axis=1, tiled=True)  146 us
    slice x1, local copies, waits for them, and re-layouts, run_stack(): w_one_b[layer_idx]  108 us
    dot_general x7, matrix products, layer_grads(): jnp.einsum('td,fd->tf', d_low, w_out, preferred_element_type=jnp.float32)  98.3 us
  transfers between devices with their start and end apart: 20, of which 19 were waited for; matrix products, arithmetic and copies ran while one was open for 11% of the time, Pallas kernels for 0%

commit v1 on v0

v1 whole, which is shorter than its diff:
```python
import functools
import math

import jax
import jax.numpy as jnp
from jax import lax
from jax.experimental import pallas as pl
from jax.experimental.pallas import tpu as pltpu
from jax.sharding import PartitionSpec as P

LEARN_RATE = 0.1
MOMENTUM = 0.9
MESH = pl.DeviceIdType.MESH
F32 = jnp.float32
BF16 = jnp.bfloat16
TILE = 256
VMEM_BYTES = 67_000_000
GELU_K = math.sqrt(2.0 / math.pi)
GELU_C = 0.044715


def place():
    me = lax.axis_index("data")
    return lax.div(me, 8), lax.rem(lax.div(me, 4), 2), lax.rem(lax.div(me, 2), 2), lax.rem(me, 2)


def index_of(z, y, x, c):
    return ((z * 2 + y) * 2 + x) * 2 + c


def ring_z(z, step):
    return lax.rem(z + step + 4, 4)


def greet(z, y, x, c):
    barrier = pltpu.get_barrier_semaphore()
    peers = [index_of(ring_z(z, k), y, x, c) for k in (1, 2, 3)]
    peers += [index_of(z, y, 1 - x, c), index_of(z, 1 - y, x, c), index_of(z, y, x, 1 - c)]
    for peer in peers:
        pl.semaphore_signal(barrier, inc=1, device_id=(peer,), device_id_type=MESH)
    pl.semaphore_wait(barrier, len(peers))


def remote(src, dst, send_sem, recv_sem, peer):
    return pltpu.make_async_remote_copy(
        src_ref=src, dst_ref=dst, send_sem=send_sem, recv_sem=recv_sem, device_id=(peer,), device_id_type=MESH
    )


def dot(a, b):
    return jnp.dot(a, b, preferred_element_type=F32)


def dot_t(a, b):
    return lax.dot_general(a, b, (((1,), (1,)), ((), ())), preferred_element_type=F32)


def whole(blocks):
    w = blocks[...]
    return w.reshape(math.prod(w.shape[:-1]), w.shape[-1])


def gelu(u):
    return (0.5 * u) * (1.0 + jnp.tanh(GELU_K * (u + GELU_C * (u * u * u))))


def forward_kernel(save, *refs):
    w1s, w2s, x_in, g1, g2, h = refs[:6]
    refs = refs[6:]
    if save:
        u_out, at_out, zt_out = refs[:3]
        refs = refs[3:]
    w1v, w2v, own_sem, load_sem, send_sem, recv_sem = refs[:6]
    if save:
        u_v, at_v, zt_v, save_sem = refs[6:]
    layers = w1s.shape[0]
    z, y, x, c = place()
    shard, full = (w1s, w2s), (g1, g2)
    tiles = x_in.shape[0] // TILE

    greet(z, y, x, c)

    def z_copy(t, l, k, from_z):
        return remote(
            shard[t].at[l], full[t].at[l, from_z, y, x, c], send_sem.at[t, l, k - 1], recv_sem.at[t, l, k - 1],
            index_of(ring_z(z, k), y, x, c),
        )

    def hop(t, s, l, arriving):
        g = full[t].at[l]
        along_x = (t == 0) == (s == 0)
        if s == 2:
            region = g.at[:, :, :, 1 - c if arriving else c]
            peer = index_of(z, y, x, 1 - c)
        else:
            xs = 1 - x if arriving and along_x else x
            ys = 1 - y if arriving and not along_x else y
            if s == 0:
                region = g.at[:, ys, xs, c]
            elif along_x:
                region = g.at[:, :, xs, c]
            else:
                region = g.at[:, ys, :, c]
            peer = index_of(z, y, 1 - x, c) if along_x else index_of(z, 1 - y, x, c)
        return remote(region, region, send_sem.at[t, l, 3 + s], recv_sem.at[t, l, 3 + s], peer)

    own = [pltpu.make_async_copy(shard[t], full[t].at[:, z, y, x, c], own_sem.at[t]) for t in (0, 1)]
    for copy in own:
        copy.start()

    def send_z(l, carry):
        for t in (0, 1):
            for k in (1, 2, 3):
                z_copy(t, l, k, z).start()
        return carry

    lax.fori_loop(0, layers, send_z, 0)
    h[...] = x_in[...].astype(F32)
    for copy in own:
        copy.wait()

    def u_save(l, rows, m):
        return pltpu.make_async_copy(u_v.at[rows], u_out.at[l, rows], save_sem.at[m])

    def at_save(l):
        return pltpu.make_async_copy(at_v, at_out.at[l], save_sem.at[tiles])

    def zt_save(l):
        return pltpu.make_async_copy(zt_v, zt_out.at[l], save_sem.at[tiles + 1])

    def compute(l):
        load1 = pltpu.make_async_copy(g1.at[l], w1v, load_sem.at[0])
        load2 = pltpu.make_async_copy(g2.at[l], w2v, load_sem.at[1])
        load1.start()
        load2.start()
        if save:
            @pl.when(l > 0)
            def _():
                at_save(l - 1).wait()
                zt_save(l - 1).wait()
        load1.wait()
        load2.wait()

        def tile(m, carry):
            start = pl.multiple_of(m * TILE, TILE)
            rows = pl.ds(start, TILE)
            a = h[rows, :].astype(BF16)
            u = dot(a, whole(w1v))
            act = gelu(u).astype(BF16)
            if save:
                @pl.when(l > 0)
                def _():
                    u_save(l - 1, rows, m).wait()
                u_v[rows, :] = u
                u_save(l, rows, m).start()
                at_v[:, rows] = a.T
                zt_v[:, rows] = act.T
            h[rows, :] += dot(act, whole(w2v))
            return carry

        lax.fori_loop(0, tiles, tile, 0)
        if save:
            at_save(l).start()
            zt_save(l).start()

    def step(it, carry):
        l = it - 3

        @pl.when(l + 3 < layers)
        def _():
            for t in (0, 1):
                for k in (1, 2, 3):
                    z_copy(t, l + 3, k, ring_z(z, -k)).wait_recv()
                hop(t, 0, l + 3, False).start()

        @pl.when((l + 2 >= 0) & (l + 2 < layers))
        def _():
            for t in (0, 1):
                hop(t, 0, l + 2, True).wait_recv()
                hop(t, 1, l + 2, False).start()

        @pl.when(l >= 0)
        def _():
            for t in (0, 1):
                hop(t, 2, l, True).wait_recv()
            compute(l)

        @pl.when((l + 1 >= 0) & (l + 1 < layers))
        def _():
            for t in (0, 1):
                hop(t, 1, l + 1, True).wait_recv()
                hop(t, 2, l + 1, False).start()

        return carry

    lax.fori_loop(0, layers + 3, step, 0)

    def drain(l, carry):
        for t in (0, 1):
            for k in (1, 2, 3):
                z_copy(t, l, k, z).wait_send()
            for s in (0, 1, 2):
                hop(t, s, l, False).wait_send()
        return carry

    lax.fori_loop(0, layers, drain, 0)
    if save:
        for m in range(tiles):
            u_save(layers - 1, pl.ds(m * TILE, TILE), m).wait()
        at_save(layers - 1).wait()
        zt_save(layers - 1).wait()


def forward(save, ident, w1s, w2s, x_in):
    layers, r1, d_ff = w1s.shape
    r2 = w2s.shape[1]
    tok, d_model = x_in.shape
    tiles = tok // TILE
    sds = jax.ShapeDtypeStruct
    hbm, vmem = pl.BlockSpec(memory_space=pl.ANY), pl.BlockSpec(memory_space=pltpu.VMEM)
    outs = [sds((layers, 4, 2, 2, 2, r1, d_ff), BF16), sds((layers, 4, 2, 2, 2, r2, d_model), BF16), sds((tok, d_model), F32)]
    out_specs = [hbm, hbm, vmem]
    scratch = [
        pltpu.VMEM((4, 2, 2, 2, r1, d_ff), BF16),
        pltpu.VMEM((4, 2, 2, 2, r2, d_model), BF16),
        pltpu.SemaphoreType.DMA((2,)),
        pltpu.SemaphoreType.DMA((2,)),
        pltpu.SemaphoreType.DMA((2, layers, 6)),
        pltpu.SemaphoreType.DMA((2, layers, 6)),
    ]
    if save:
        outs += [sds((layers, tok, d_ff), F32), sds((layers, d_model, tok), BF16), sds((layers, d_ff, tok), BF16)]
        out_specs += [hbm, hbm, hbm]
        scratch += [
            pltpu.VMEM((tok, d_ff), F32),
            pltpu.VMEM((d_model, tok), BF16),
            pltpu.VMEM((d_ff, tok), BF16),
            pltpu.SemaphoreType.DMA((tiles + 2,)),
        ]
    return pl.pallas_call(
        functools.partial(forward_kernel, save),
        out_shape=outs,
        in_specs=[vmem, vmem, vmem],
        out_specs=out_specs,
        scratch_shapes=scratch,
        compiler_params=pltpu.CompilerParams(collective_id=ident, has_side_effects=True, vmem_limit_bytes=VMEM_BYTES),
        name="forward_save" if save else "forward_last",
    )(w1s, w2s, x_in)


def gelu_back(u, q):
    t = jnp.tanh(GELU_K * (u + GELU_C * (u * u * u)))
    slope = 0.5 * (1.0 + t) + (0.5 * GELU_K) * u * (1.0 - t * t) * (1.0 + (3.0 * GELU_C) * (u * u))
    return slope * q


def backward_kernel(*refs):
    g1, g2, u_in, at_in, zt_in, d_in, s1, s2, d, d_low, w1v, w2v, u_v, at_v, zt_v, r_v = refs[:16]
    bufs = (refs[16:24], refs[24:32])
    load_sem, send_sem, recv_sem, free_sem = refs[32:]
    sums = (s1, s2)
    layers = s1.shape[0]
    z, y, x, c = place()
    tok = d.shape[0]
    tiles = tok // TILE

    greet(z, y, x, c)

    x_peer, y_peer, core_peer = index_of(z, y, 1 - x, c), index_of(z, 1 - y, x, c), index_of(z, y, x, 1 - c)

    def peer_of(t, s):
        if s == 0:
            return core_peer
        return y_peer if (t == 0) == (s == 1) else x_peer

    def exchange(t, s):
        grad, got0, part, got1, quart, got2, line, got3 = bufs[t]
        if s == 0:
            src, dst = grad.at[:, :, :, 1 - c], got0
        elif s == 1:
            src, dst = (part.at[:, 1 - y] if t == 0 else part.at[:, :, 1 - x]), got1
        else:
            src, dst = quart.at[:, 1 - x if t == 0 else 1 - y], got2
        return remote(src, dst, send_sem.at[t, s], recv_sem.at[t, s], peer_of(t, s))

    def line_send(t, k):
        line, got3 = bufs[t][6], bufs[t][7]
        to = ring_z(z, k)
        return remote(line.at[to], got3.at[k - 1], send_sem.at[t, 2 + k], recv_sem.at[t, 2 + k], index_of(to, y, x, c))

    def give(l, sem, peer):
        @pl.when(l > 0)
        def _():
            pl.semaphore_signal(sem, inc=1, device_id=(peer,), device_id_type=MESH)

    def take(l, sem):
        @pl.when(l < layers - 1)
        def _():
            pl.semaphore_wait(sem, 1)

    def send(t, s, l):
        take(l, free_sem.at[t, s])
        exchange(t, s).start()

    def add(a, b):
        return (a.astype(F32) + b.astype(F32)).astype(BF16)

    def finish(t, l):
        line, got3 = bufs[t][6], bufs[t][7]
        for k in (1, 2, 3):
            line_send(t, k).wait_recv()
        total = line[z].astype(F32) + got3[0].astype(F32) + got3[1].astype(F32) + got3[2].astype(F32)
        sums[t][l] = total.astype(BF16)
        for k in (1, 2, 3):
            line_send(t, k).wait_send()
            give(l, free_sem.at[t, 2 + k], index_of(ring_z(z, -k), y, x, c))

    def to_line(t, l):
        quart, got2, line = bufs[t][4:7]
        exchange(t, 2).wait_recv()
        mine = x if t == 0 else y
        for zz in range(4):
            line[zz] = add(quart[zz, mine], got2[zz])
        exchange(t, 2).wait_send()
        give(l, free_sem.at[t, 2], peer_of(t, 2))
        for k in (1, 2, 3):
            take(l, free_sem.at[t, 2 + k])
            line_send(t, k).start()

    def to_quart(t, l):
        part, got1, quart = bufs[t][2:5]
        exchange(t, 1).wait_recv()

        def body(zz, carry):
            for j in (0, 1):
                own = part[zz, y, j] if t == 0 else part[zz, j, x]
                quart[zz, j] = add(own, got1[zz, j])
            return carry

        lax.fori_loop(0, 4, body, 0)
        exchange(t, 1).wait_send()
        give(l, free_sem.at[t, 1], peer_of(t, 1))
        send(t, 2, l)

    def to_part(t, l):
        grad, got0, part = bufs[t][:3]
        exchange(t, 0).wait_recv()

        def body(zz, carry):
            for yy in (0, 1):
                for xx in (0, 1):
                    part[zz, yy, xx] = add(grad[zz, yy, xx, c], got0[zz, yy, xx])
            return carry

        lax.fori_loop(0, 4, body, 0)
        exchange(t, 0).wait_send()
        give(l, free_sem.at[t, 0], peer_of(t, 0))
        send(t, 1, l)

    loads = (
        (lambda l: g1.at[l], w1v),
        (lambda l: g2.at[l], w2v),
        (lambda l: u_in.at[l], u_v),
        (lambda l: at_in.at[l], at_v),
        (lambda l: zt_in.at[l], zt_v),
    )

    def load(n, l):
        return pltpu.make_async_copy(loads[n][0](l), loads[n][1], load_sem.at[n])

    def prefetch(n, l):
        @pl.when(l > 0)
        def _():
            load(n, l - 1).start()

    def put(t, zz, res):
        grad = bufs[t][0]
        rows = grad.shape[4]
        for k in range(8):
            grad[zz, k // 4, k // 2 % 2, k % 2] = res[k * rows:(k + 1) * rows].astype(BF16)

    def compute(l):
        d_low[...] = d[...].astype(BF16)
        load(4, l).wait()

        def grad_two(zz, carry):
            step = d_two // 4
            put(1, zz, dot(zt_v[pl.ds(pl.multiple_of(zz * step, step), step), :], d_low[...]))
            return carry

        d_two = zt_v.shape[0]
        lax.fori_loop(0, 4, grad_two, 0)
        send(1, 0, l)
        prefetch(4, l)
        load(1, l).wait()
        load(2, l).wait()

        def pre(m, carry):
            rows = pl.ds(pl.multiple_of(m * TILE, TILE), TILE)
            q = dot_t(d_low[rows, :], whole(w2v))
            r_v[rows, :] = gelu_back(u_v[rows, :], q).astype(BF16)
            return carry

        lax.fori_loop(0, tiles, pre, 0)
        prefetch(1, l)
        prefetch(2, l)
        load(3, l).wait()

        def grad_one(zz, carry):
            step = at_v.shape[0] // 4
            put(0, zz, dot(at_v[pl.ds(pl.multiple_of(zz * step, step), step), :], r_v[...]))
            return carry

        lax.fori_loop(0, 4, grad_one, 0)
        send(0, 0, l)
        prefetch(3, l)
        load(0, l).wait()

        @pl.when(l > 0)
        def _():
            def back(m, carry):
                rows = pl.ds(pl.multiple_of(m * TILE, TILE), TILE)
                d[rows, :] += dot_t(r_v[rows, :], whole(w1v))
                return carry

            lax.fori_loop(0, tiles, back, 0)

        prefetch(0, l)

    first = pltpu.make_async_copy(d_in, d, load_sem.at[len(loads)])
    first.start()
    for n in range(len(loads)):
        load(n, layers - 1).start()
    first.wait()

    def step(it, carry):
        l = layers - 1 - it
        for lag, stage in ((4, finish), (3, to_line), (2, to_quart), (1, to_part)):
            @pl.when((l + lag >= 0) & (l + lag < layers))
            def _():
                for t in (1, 0):
                    stage(t, l + lag)

        @pl.when(l >= 0)
        def _():
            compute(l)

        return carry

    lax.fori_loop(0, layers + 4, step, 0)


def backward(ident, g1, g2, u_all, at_all, zt_all, d_state):
    layers, r1, d_ff = g1.shape[0], g1.shape[5], g1.shape[6]
    r2 = g2.shape[5]
    tok, d_model = d_state.shape
    sds = jax.ShapeDtypeStruct
    hbm, vmem = pl.BlockSpec(memory_space=pl.ANY), pl.BlockSpec(memory_space=pltpu.VMEM)
    scratch = [
        pltpu.VMEM((tok, d_model), F32),
        pltpu.VMEM((tok, d_model), BF16),
        pltpu.VMEM((4, 2, 2, 2, r1, d_ff), BF16),
        pltpu.VMEM((4, 2, 2, 2, r2, d_model), BF16),
        pltpu.VMEM((tok, d_ff), F32),
        pltpu.VMEM((d_model, tok), BF16),
        pltpu.VMEM((d_ff, tok), BF16),
        pltpu.VMEM((tok, d_ff), BF16),
    ]
    for block in ((r1, d_ff), (r2, d_model)):
        for lead in ((4, 2, 2, 2), (4, 2, 2), (4, 2, 2), (4, 2), (4, 2), (4,), (4,), (3,)):
            scratch.append(pltpu.VMEM(lead + block, BF16))
    scratch += [
        pltpu.SemaphoreType.DMA((6,)),
        pltpu.SemaphoreType.DMA((2, 6)),
        pltpu.SemaphoreType.DMA((2, 6)),
        pltpu.SemaphoreType.REGULAR((2, 6)),
    ]
    return pl.pallas_call(
        backward_kernel,
        out_shape=[sds((layers, r1, d_ff), BF16), sds((layers, r2, d_model), BF16)],
        in_specs=[hbm] * 6,
        out_specs=[vmem, vmem],
        scratch_shapes=scratch,
        compiler_params=pltpu.CompilerParams(collective_id=ident, has_side_effects=True, vmem_limit_bytes=VMEM_BYTES),
        name="backward",
    )(g1, g2, u_all, at_all, zt_all, d_state)


def solution(mesh):
    n_dev = mesh.shape["data"]
    w_spec = P(None, "data", None)
    row_spec = P("data", None)

    def device_step(w_one, w_two, mom_one, mom_two, x_zero, y_zero, x_one, y_one):
        tok_dev, d_model = x_zero.shape
        g1, g2, h_end, u_all, at_all, zt_all = forward(True, 0, w_one.astype(BF16), w_two.astype(BF16), x_zero)
        d_state = (h_end - y_zero.astype(F32)) / (n_dev * tok_dev * d_model)
        sum_one, sum_two = backward(1, g1, g2, u_all, at_all, zt_all, d_state)
        new_mom_one = MOMENTUM * mom_one + sum_one.astype(F32)
        new_mom_two = MOMENTUM * mom_two + sum_two.astype(F32)
        new_w_one = w_one - LEARN_RATE * new_mom_one
        new_w_two = w_two - LEARN_RATE * new_mom_two
        h_last = forward(False, 2, new_w_one.astype(BF16), new_w_two.astype(BF16), x_one)[2]
        loss_rows = jnp.sum(jnp.square(h_last - y_one.astype(F32)), axis=1) / (2 * d_model)
        return new_w_one, new_w_two, new_mom_one, new_mom_two, loss_rows, h_last

    return jax.shard_map(device_step, mesh=mesh, in_specs=(w_spec, w_spec, w_spec, w_spec, row_spec, row_spec, row_spec, row_spec), out_specs=(w_spec, w_spec, w_spec, w_spec, P("data"), row_spec), check_vma=False)
```

time: 2750 us -> 825 us (0.30)
  waiting for transfers between devices: 2020 us -> 0 us
  Pallas kernels: 0 us -> 788 us
  matrix products: 545 us -> 0 us
  local copies, waits for them, and re-layouts: 146 us -> 1.69 us
    reduce_scatter x16 -> x0, waiting for transfers between devices: 1530 us -> none  [the longest x8 835 us: device_step(): lax.psum_scatter(grad_out, 'data', scatter_dimension=0, tiled=True)]
    pallas_call x0 -> x3, Pallas kernels: none -> 788 us  [the longest x2 530 us: forward(): pl.pallas_call(functools.partial(forward_kernel, save), out_shape=outs, i...]
    dot_general x54 -> x0, matrix products: 545 us -> none  [the longest x16 189 us: run_stack(): jnp.dot(hidden, w_two_b[layer_idx], preferred_element_type=jnp.float32)]
    all_gather x4 -> x0, waiting for transfers between devices: 496 us -> none  [the longest x1 153 us: device_step(): lax.all_gather(w_one.astype(jnp.bfloat16), 'data', axis=1, tiled=True)]
    slice x1 -> x0, local copies, waits for them, and re-layouts: 108 us -> none  [run_stack(): w_one_b[layer_idx]]
    unnamed x86 -> x11, local copies, waits for them, and re-layouts: 34.1 us -> 1.69 us
  transfers between devices with their start and end apart: 20 -> 0, of which waited for: 19 -> 0; matrix products, arithmetic and copies ran while one was open for 11% -> 0% of each run, Pallas kernels for 0% -> 0%
where the time goes in v1:
time: 825 us; the launch traced here: 809 us
  Pallas kernels  788 us (96%)
  other arithmetic  18.7 us (2%)
    pallas_call x2, Pallas kernels, forward(): pl.pallas_call(functools.partial(forward_kernel, save), out_shape=outs, i...  530 us
    pallas_call x1, Pallas kernels, backward(): pl.pallas_call(backward_kernel, out_shape=[sds((layers, r1, d_ff), BF16),...  258 us

profile of v1, /device:TPU:17, one launch (start us, length us, event | category | flops | bytes accessed | tf_op | source)
XLA Modules:
  0.0 808.8 jit_solution(12565234154932945948)
XLA Ops:
  0.6 0.0 copy-start.1
  0.6 2.5 convert_element_type.24.refs_0_
  3.2 0.0 copy-done.1
  3.2 1.0 convert_element_type.25.refs_1_
  4.1 270.7 %forward_save.1 = (bf16[8,4,2,2,2,24,2048]{6,5,4,3,2,1,0:T(8,128)(2,1)}, bf16[8,4,2,2,2,64,768]{6,5,4,3,2,1,0:T(8,128)(2,1)}, f32[1024,768]{1,0:T(8,128)}, f32[8...) custom-call(bf16[8,24,2048]{2,1,0:T(8,128)(2,1)} %convert_element_type.24.refs_0_, ...), custom_call_target="tpu_custom_call" | custom-call | tf_op jit(solution)/shard_map/forward_save/pallas_call | solution.py:240
  274.8 4.4 subtract_multiply_fusion.refs_5_
  279.2 258.2 %backward.1 = (bf16[8,24,2048]{2,1,0:T(8,128)(2,1)}, bf16[8,64,768]{2,1,0:T(8,128)(2,1)}) custom-call(bf16[8,4,2,2,2,24,2048]{6,5,4,3,2,1,0:T(8,128)(2,1)} %get-tuple-element.15.refs_0_, bf16[8,4,2,2,2,64,768]{6,5,4,3,2,1,0:T(8,128)(2,1)} %get-tuple-element.16.refs_1_, f32[8,1024,2048]{2,1,0:T(8,128)} %get-tuple-element.17.refs_2_, ...), custom_call_target="tpu_custom_call" | custom-call | tf_op jit(solution)/shard_map/backward/pallas_call | solution.py:478
  537.4 0.0 copy-start.2
  537.4 0.0 copy-start.3
  537.4 0.0 copy-start.4
  537.4 4.9 fusion.1
  542.2 0.0 copy-done.2
  542.2 0.0 copy-done.3
  542.2 0.0 copy-done.4
  542.3 2.4 fusion
  544.7 258.9 %forward_last.1 = (bf16[8,4,2,2,2,24,2048]{6,5,4,3,2,1,0:T(8,128)(2,1)}, bf16[8,4,2,2,2,64,768]{6,5,4,3,2,1,0:T(8,128)(2,1)}, f32[1024,768]{1,0:T(8,128)}) custom-call(bf16[8,24,2048]{2,1,0:T(8,128)(2,1)} %get-tuple-element.27.refs_0_, bf16[8,64,768]{2,1,0:T(8,128)(2,1)} %get-tuple-element.24.refs_1_, bf16[1024,768]{1,0:T(8,128)(2,1)} %refs_2_.3), custom_call_target="tpu_custom_call" | custom-call | tf_op jit(solution)/shard_map/forward_last/pallas_call | solution.py:240
  803.6 0.0 copy-start
  803.6 3.0 multiply_reduce_fusion
  806.6 0.6 broadcast_multiply_fusion
  807.2 0.0 copy-done
  807.2 1.7 copy.15
Async XLA Ops:
  0.6 2.5 copy-start.1
  537.4 4.9 copy-start.2
  537.4 4.9 copy-start.3
  537.4 4.9 copy-start.4
  803.6 3.6 copy-start

commit v2 on v1

--- a/solution.py
+++ b/solution.py
@@ -14,6 +14,8 @@
 F32 = jnp.float32
 BF16 = jnp.bfloat16
 TILE = 256
+AHEAD = 5
+LINE_AT = 0
 VMEM_BYTES = 67_000_000
 GELU_K = math.sqrt(2.0 / math.pi)
 GELU_C = 0.044715
@@ -64,60 +66,137 @@
     return (0.5 * u) * (1.0 + jnp.tanh(GELU_K * (u + GELU_C * (u * u * u))))
 
 
-def forward_kernel(save, *refs):
-    w1s, w2s, x_in, g1, g2, h = refs[:6]
-    refs = refs[6:]
+def forward_kernel(save, scale, *refs):
+    w1f, w2f, x_in, y_in = refs[:4] if save else refs[:3] + (None,)
+    g1, g2, h = refs[4:7] if save else refs[3:6]
+    refs = refs[7:] if save else refs[6:]
     if save:
         u_out, at_out, zt_out = refs[:3]
         refs = refs[3:]
-    w1v, w2v, own_sem, load_sem, send_sem, recv_sem = refs[:6]
+    w1s, w2s = refs[:2]
+    refs = refs[2:]
+    far = 6 if save else 5
+    w1v, w2v, own_sem, load_sem, send_sem, recv_sem, line_sems = refs[:7]
     if save:
-        u_v, at_v, zt_v, save_sem = refs[6:]
+        u_v, at_v, zt_v, save_sem = refs[7:]
     layers = w1s.shape[0]
     z, y, x, c = place()
     shard, full = (w1s, w2s), (g1, g2)
     tiles = x_in.shape[0] // TILE
+    w1s[...] = w1f[...].astype(BF16)
+    w2s[...] = w2f[...].astype(BF16)
 
     greet(z, y, x, c)
 
     def z_copy(t, l, k, from_z):
         return remote(
-            shard[t].at[l], full[t].at[l, from_z, y, x, c], send_sem.at[t, l, k - 1], recv_sem.at[t, l, k - 1],
+            shard[t].at[l], full[t].at[l, from_z, y, x, c], send_sem.at[t, k - 1], recv_sem.at[t, l, k - 1],
             index_of(ring_z(z, k), y, x, c),
         )
 
+    def half(t, l, other, core):
+        g = full[t].at[l]
+        if t == 0:
+            return g.at[:, 1 - y if other else y, :, core]
+        return g.at[:, :, 1 - x if other else x, core]
+
     def hop(t, s, l, arriving):
-        g = full[t].at[l]
-        along_x = (t == 0) == (s == 0)
-        if s == 2:
-            region = g.at[:, :, :, 1 - c if arriving else c]
+        if s == 1:
+            region = half(t, l, arriving, c)
+            peer = index_of(z, 1 - y, x, c) if t == 0 else index_of(z, y, 1 - x, c)
+        else:
+            region = half(t, l, s == 3, 1 - c if arriving else c)
             peer = index_of(z, y, x, 1 - c)
+        return remote(region, region, send_sem.at[t, 3 + s], recv_sem.at[t, l, 3 + s], peer)
+
+    def first(t, l, k):
+        region = full[t].at[l, ring_z(z, -k), y, x, c]
+        src = region if k else shard[t].at[l]
+        peer = index_of(z, y, 1 - x, c) if t == 0 else index_of(z, 1 - y, x, c)
+        return remote(src, region, send_sem.at[t, 3], recv_sem.at[t, l, 3 if k else 7], peer)
+
+    def first_arrived(t, l):
+        first(t, l, 0).wait_recv()
+        region = full[t].at[l, 0:3, y, x, c]
+        remote(region, region, send_sem.at[t, 3], recv_sem.at[t, l, 3], index_of(z, y, x, 1 - c)).wait_recv()
+
+    def plane(p, t, arriving):
+        along_x = (t == 0) == (p == 0)
+        xs = 1 - x if arriving and along_x else x
+        ys = 1 - y if arriving and not along_x else y
+        g = full[t].at[far, z]
+        if p == 0:
+            region = g.at[ys, xs, c]
         else:
-            xs = 1 - x if arriving and along_x else x
-            ys = 1 - y if arriving and not along_x else y
-            if s == 0:
-                region = g.at[:, ys, xs, c]
-            elif along_x:
-                region = g.at[:, :, xs, c]
-            else:
-                region = g.at[:, ys, :, c]
-            peer = index_of(z, y, 1 - x, c) if along_x else index_of(z, 1 - y, x, c)
-        return remote(region, region, send_sem.at[t, l, 3 + s], recv_sem.at[t, l, 3 + s], peer)
+            region = g.at[:, xs, c] if along_x else g.at[ys, :, c]
+        src = region if p or arriving else shard[t].at[far]
+        peer = index_of(z, y, 1 - x, c) if along_x else index_of(z, 1 - y, x, c)
+        return remote(src, region, send_sem.at[t, 7 + p], recv_sem.at[t, far, p], peer)
+
+    def line(j, t, way, arriving):
+        region = full[t].at[far, z - way * (j if arriving else j - 1), :, :, c]
+        n = 2 * j - 2 + (way > 0)
+        return remote(region, region, line_sems.at[0, t, n], line_sems.at[1, t, n], index_of(z + way, y, x, c))
+
+    def skip_far(n):
+        return jnp.where(n < far, n, n + 1)
+
+    def within(zz):
+        return (zz >= 0) & (zz < 4)
+
+    def line_step(j):
+        for t in (0, 1):
+            for way in (1, -1):
+                if j > 1:
+                    @pl.when(within(z - way * (j - 1)))
+                    def _():
+                        line(j - 1, t, way, True).wait_recv()
+                if j < 4:
+                    @pl.when(within(z - way * (j - 1)) & within(z + way))
+                    def _():
+                        line(j, t, way, False).start()
+
+    def send_z(l, carry):
+        @pl.when(l != far)
+        def _():
+            for t in (0, 1):
+                for k in (1, 2, 3):
+                    z_copy(t, l, k, z).start()
+        return carry
+
+    def send_own(l, carry):
+        @pl.when(l != far)
+        def _():
+            for t in (0, 1):
+                first(t, l, 0).start()
+        return carry
+
+    def z_to_first(t, l):
+        for k in (1, 2, 3):
+            z_copy(t, l, k, ring_z(z, -k)).wait_recv()
+            first(t, l, k).start()
+
+    def to_plane(t, l):
+        first_arrived(t, l)
+        hop(t, 1, l, False).start()
+        hop(t, 2, l, False).start()
+
+    def to_core(t, l):
+        hop(t, 1, l, True).wait_recv()
+        hop(t, 3, l, False).start()
 
     own = [pltpu.make_async_copy(shard[t], full[t].at[:, z, y, x, c], own_sem.at[t]) for t in (0, 1)]
+    for t in (0, 1):
+        plane(0, t, False).start()
+    lax.fori_loop(0, AHEAD, send_z, 0)
+    lax.fori_loop(0, layers, send_own, 0)
     for copy in own:
         copy.start()
-
-    def send_z(l, carry):
-        for t in (0, 1):
-            for k in (1, 2, 3):
-                z_copy(t, l, k, z).start()
-        return carry
-
-    lax.fori_loop(0, layers, send_z, 0)
     h[...] = x_in[...].astype(F32)
-    for copy in own:
-        copy.wait()
+    for t in (0, 1):
+        own[t].wait()
+        plane(0, t, True).wait_recv()
+        plane(1, t, False).start()
 
     def u_save(l, rows, m):
         return pltpu.make_async_copy(u_v.at[rows], u_out.at[l, rows], save_sem.at[m])
@@ -163,57 +242,89 @@
             at_save(l).start()
             zt_save(l).start()
 
-    def step(it, carry):
-        l = it - 3
-
-        @pl.when(l + 3 < layers)
+    for stage in (z_to_first, to_plane):
+        for t in (0, 1):
+            stage(t, 0)
+    for l in (1, 2):
+        for t in (0, 1):
+            z_to_first(t, l)
+    for t in (0, 1):
+        to_plane(t, 1)
+    for t in (0, 1):
+        to_core(t, 0)
+
+    def step(l, carry):
+        @pl.when(l + AHEAD < layers)
+        def _():
+            send_z(l + AHEAD, 0)
+
+        third, second = skip_far(l + 3), skip_far(l + 2)
+
+        @pl.when(third < layers)
         def _():
             for t in (0, 1):
-                for k in (1, 2, 3):
-                    z_copy(t, l + 3, k, ring_z(z, -k)).wait_recv()
-                hop(t, 0, l + 3, False).start()
-
-        @pl.when((l + 2 >= 0) & (l + 2 < layers))
+                z_to_first(t, third)
+
+        @pl.when(second < layers)
         def _():
             for t in (0, 1):
-                hop(t, 0, l + 2, True).wait_recv()
-                hop(t, 1, l + 2, False).start()
-
-        @pl.when(l >= 0)
+                to_plane(t, second)
+
+        for j in (1, 2, 3, 4):
+            @pl.when(l == LINE_AT + j)
+            def _():
+                if j == 1:
+                    for t in (0, 1):
+                        plane(1, t, True).wait_recv()
+                line_step(j)
+
+        for t in (0, 1):
+            hop(t, 2, l, True).wait_recv()
+            hop(t, 3, l, True).wait_recv()
+        compute(l)
+
+        @pl.when(l + 1 < layers)
         def _():
             for t in (0, 1):
-                hop(t, 2, l, True).wait_recv()
-            compute(l)
-
-        @pl.when((l + 1 >= 0) & (l + 1 < layers))
-        def _():
-            for t in (0, 1):
-                hop(t, 1, l + 1, True).wait_recv()
-                hop(t, 2, l + 1, False).start()
+                @pl.when(l + 1 != far)
+                def _():
+                    to_core(t, l + 1)
+
+                @pl.when(l + 1 == far)
+                def _():
+                    hop(t, 2, far, False).start()
+                    hop(t, 3, far, False).start()
 
         return carry
 
-    lax.fori_loop(0, layers + 3, step, 0)
-
-    def drain(l, carry):
-        for t in (0, 1):
-            for k in (1, 2, 3):
-                z_copy(t, l, k, z).wait_send()
-            for s in (0, 1, 2):
-                hop(t, s, l, False).wait_send()
-        return carry
-
-    lax.fori_loop(0, layers, drain, 0)
+    lax.fori_loop(0, layers, step, 0)
+
+    others = pl.ds(0, layers - 1)
+    for t in (0, 1):
+        f = full[t]
+        sent = [f.at[others, z, y, x, c]] * 3
+        sent += [f.at[others, :, y, x, c], f.at[others, :, y, :, c] if t == 0 else f.at[others, :, :, x, c]]
+        sent += [f.at[:, :, y, :, c] if t == 0 else f.at[:, :, :, x, c]] * 2
+        for n, region in enumerate(sent):
+            remote(region, region, send_sem.at[t, n], recv_sem.at[t, 0, 0], index_of(z, y, x, 1 - c)).wait_send()
+        for p in (0, 1):
+            plane(p, t, False).wait_send()
+        for j in (1, 2, 3):
+            for way in (1, -1):
+                @pl.when(within(z - way * (j - 1)) & within(z + way))
+                def _():
+                    line(j, t, way, False).wait_send()
     if save:
         for m in range(tiles):
             u_save(layers - 1, pl.ds(m * TILE, TILE), m).wait()
+        h[...] = (h[...] - y_in[...].astype(F32)) / scale
         at_save(layers - 1).wait()
         zt_save(layers - 1).wait()
 
 
-def forward(save, ident, w1s, w2s, x_in):
-    layers, r1, d_ff = w1s.shape
-    r2 = w2s.shape[1]
+def forward(save, ident, w1f, w2f, x_in, y_in=None, scale=None):
+    layers, r1, d_ff = w1f.shape
+    r2 = w2f.shape[1]
     tok, d_model = x_in.shape
     tiles = tok // TILE
     sds = jax.ShapeDtypeStruct
@@ -221,12 +332,15 @@
     outs = [sds((layers, 4, 2, 2, 2, r1, d_ff), BF16), sds((layers, 4, 2, 2, 2, r2, d_model), BF16), sds((tok, d_model), F32)]
     out_specs = [hbm, hbm, vmem]
     scratch = [
+        pltpu.VMEM((layers, r1, d_ff), BF16),
+        pltpu.VMEM((layers, r2, d_model), BF16),
         pltpu.VMEM((4, 2, 2, 2, r1, d_ff), BF16),
         pltpu.VMEM((4, 2, 2, 2, r2, d_model), BF16),
         pltpu.SemaphoreType.DMA((2,)),
         pltpu.SemaphoreType.DMA((2,)),
-        pltpu.SemaphoreType.DMA((2, layers, 6)),
-        pltpu.SemaphoreType.DMA((2, layers, 6)),
+        pltpu.SemaphoreType.DMA((2, 9)),
+        pltpu.SemaphoreType.DMA((2, layers, 8)),
+        pltpu.SemaphoreType.DMA((2, 2, 6)),
     ]
     if save:
         outs += [sds((layers, tok, d_ff), F32), sds((layers, d_model, tok), BF16), sds((layers, d_ff, tok), BF16)]
@@ -238,14 +352,14 @@
             pltpu.SemaphoreType.DMA((tiles + 2,)),
         ]
     return pl.pallas_call(
-        functools.partial(forward_kernel, save),
+        functools.partial(forward_kernel, save, scale),
         out_shape=outs,
-        in_specs=[vmem, vmem, vmem],
+        in_specs=[vmem] * (4 if save else 3),
         out_specs=out_specs,
         scratch_shapes=scratch,
         compiler_params=pltpu.CompilerParams(collective_id=ident, has_side_effects=True, vmem_limit_bytes=VMEM_BYTES),
         name="forward_save" if save else "forward_last",
-    )(w1s, w2s, x_in)
+    )(w1f, w2f, x_in, *([y_in] if save else []))
 
 
 def gelu_back(u, q):
@@ -257,7 +371,8 @@
 def backward_kernel(*refs):
     g1, g2, u_in, at_in, zt_in, d_in, s1, s2, d, d_low, w1v, w2v, u_v, at_v, zt_v, r_v = refs[:16]
     bufs = (refs[16:24], refs[24:32])
-    load_sem, send_sem, recv_sem, free_sem = refs[32:]
+    late = (refs[32:35], refs[35:38])
+    load_sem, send_sem, recv_sem, free_sem = refs[38:]
     sums = (s1, s2)
     layers = s1.shape[0]
     z, y, x, c = place()
@@ -277,11 +392,18 @@
         grad, got0, part, got1, quart, got2, line, got3 = bufs[t]
         if s == 0:
             src, dst = grad.at[:, :, :, 1 - c], got0
-        elif s == 1:
+        else:
             src, dst = (part.at[:, 1 - y] if t == 0 else part.at[:, :, 1 - x]), got1
+        return remote(src, dst, send_sem.at[t, s], recv_sem.at[t, s], peer_of(t, s))
+
+    def trade(t, k):
+        if k == 0:
+            src, dst = late[t][0], late[t][1]
         else:
-            src, dst = quart.at[:, 1 - x if t == 0 else 1 - y], got2
-        return remote(src, dst, send_sem.at[t, s], recv_sem.at[t, s], peer_of(t, s))
+            quart, got2 = bufs[t][4], bufs[t][5]
+            to = ring_z(z, k)
+            src, dst = quart.at[to, 1 - x if t == 0 else 1 - y], got2.at[to]
+        return remote(src, dst, send_sem.at[t, 6 + k], recv_sem.at[t, 6 + k], peer_of(t, 2))
 
     def line_send(t, k):
         line, got3 = bufs[t][6], bufs[t][7]
@@ -309,19 +431,22 @@
         line, got3 = bufs[t][6], bufs[t][7]
         for k in (1, 2, 3):
             line_send(t, k).wait_recv()
-        total = line[z].astype(F32) + got3[0].astype(F32) + got3[1].astype(F32) + got3[2].astype(F32)
-        sums[t][l] = total.astype(BF16)
+        late[t][2][l] += got3[0].astype(F32) + got3[1].astype(F32) + got3[2].astype(F32)
         for k in (1, 2, 3):
             line_send(t, k).wait_send()
             give(l, free_sem.at[t, 2 + k], index_of(ring_z(z, -k), y, x, c))
 
     def to_line(t, l):
         quart, got2, line = bufs[t][4:7]
-        exchange(t, 2).wait_recv()
+        for k in (1, 2, 3):
+            trade(t, k).wait_recv()
         mine = x if t == 0 else y
-        for zz in range(4):
-            line[zz] = add(quart[zz, mine], got2[zz])
-        exchange(t, 2).wait_send()
+        for k in (1, 2, 3):
+            to = ring_z(z, k)
+            line[to] = add(quart[to, mine], got2[to])
+        late[t][2][l] = quart[z, mine].astype(F32)
+        for k in (1, 2, 3):
+            trade(t, k).wait_send()
         give(l, free_sem.at[t, 2], peer_of(t, 2))
         for k in (1, 2, 3):
             take(l, free_sem.at[t, 2 + k])
@@ -340,7 +465,10 @@
         lax.fori_loop(0, 4, body, 0)
         exchange(t, 1).wait_send()
         give(l, free_sem.at[t, 1], peer_of(t, 1))
-        send(t, 2, l)
+        take(l, free_sem.at[t, 2])
+        for k in (1, 2, 3):
+            trade(t, k).start()
+        late[t][0][l] = quart[z, 1 - x if t == 0 else 1 - y]
 
     def to_part(t, l):
         grad, got0, part = bufs[t][:3]
@@ -441,6 +569,11 @@
                 for t in (1, 0):
                     stage(t, l + lag)
 
+        @pl.when(l + 2 == 0)
+        def _():
+            for t in (0, 1):
+                trade(t, 0).start()
+
         @pl.when(l >= 0)
         def _():
             compute(l)
@@ -448,6 +581,16 @@
         return carry
 
     lax.fori_loop(0, layers + 4, step, 0)
+
+    for t in (0, 1):
+        trade(t, 0).wait()
+
+    def total(l, carry):
+        for t in (0, 1):
+            sums[t][l] = (late[t][2][l] + late[t][1][l].astype(F32)).astype(BF16)
+        return carry
+
+    lax.fori_loop(0, layers, total, 0)
 
 
 def backward(ident, g1, g2, u_all, at_all, zt_all, d_state):
@@ -469,10 +612,12 @@
     for block in ((r1, d_ff), (r2, d_model)):
         for lead in ((4, 2, 2, 2), (4, 2, 2), (4, 2, 2), (4, 2), (4, 2), (4,), (4,), (3,)):
             scratch.append(pltpu.VMEM(lead + block, BF16))
+    for block in ((r1, d_ff), (r2, d_model)):
+        scratch += [pltpu.VMEM((layers,) + block, kind) for kind in (BF16, BF16, F32)]
     scratch += [
         pltpu.SemaphoreType.DMA((6,)),
-        pltpu.SemaphoreType.DMA((2, 6)),
-        pltpu.SemaphoreType.DMA((2, 6)),
+        pltpu.SemaphoreType.DMA((2, 10)),
+        pltpu.SemaphoreType.DMA((2, 10)),
         pltpu.SemaphoreType.REGULAR((2, 6)),
     ]
     return pl.pallas_call(
@@ -493,14 +638,14 @@
 
     def device_step(w_one, w_two, mom_one, mom_two, x_zero, y_zero, x_one, y_one):
         tok_dev, d_model = x_zero.shape
-        g1, g2, h_end, u_all, at_all, zt_all = forward(True, 0, w_one.astype(BF16), w_two.astype(BF16), x_zero)
-        d_state = (h_end - y_zero.astype(F32)) / (n_dev * tok_dev * d_model)
+        scale = n_dev * tok_dev * d_model
+        g1, g2, d_state, u_all, at_all, zt_all = forward(True, 0, w_one, w_two, x_zero, y_zero, scale)
         sum_one, sum_two = backward(1, g1, g2, u_all, at_all, zt_all, d_state)
         new_mom_one = MOMENTUM * mom_one + sum_one.astype(F32)
         new_mom_two = MOMENTUM * mom_two + sum_two.astype(F32)
         new_w_one = w_one - LEARN_RATE * new_mom_one
         new_w_two = w_two - LEARN_RATE * new_mom_two
-        h_last = forward(False, 2, new_w_one.astype(BF16), new_w_two.astype(BF16), x_one)[2]
+        h_last = forward(False, 2, new_w_one, new_w_two, x_one)[2]
         loss_rows = jnp.sum(jnp.square(h_last - y_one.astype(F32)), axis=1) / (2 * d_model)
         return new_w_one, new_w_two, new_mom_one, new_mom_two, loss_rows, h_last
 

time: 825 us -> 740 us (0.90); the launches traced: 809 us -> 739 us
  Pallas kernels: 788 us -> 727 us
  other arithmetic: 18.7 us -> 10.2 us
    pallas_call x2, Pallas kernels: 530 us -> 485 us  [forward(): pl.pallas_call(functools.partial(forward_kernel, save, scale), out_shape=...]
    pallas_call x1, Pallas kernels: 258 us -> 242 us  [backward(): pl.pallas_call(backward_kernel, out_shape=[sds((layers, r1, d_ff), BF16),...]
    convert_element_type x4 -> x0, other arithmetic: 10.7 us -> none  [the longest x1 4.85 us: device_step(): new_w_one.astype(BF16)]
where the time goes in v2:
time: 740 us; the launch traced here: 739 us
  Pallas kernels  727 us (98%)
  other arithmetic  10.2 us (1%)
    pallas_call x2, Pallas kernels, forward(): pl.pallas_call(functools.partial(forward_kernel, save, scale), out_shape=...  485 us
    pallas_call x1, Pallas kernels, backward(): pl.pallas_call(backward_kernel, out_shape=[sds((layers, r1, d_ff), BF16),...  242 us

profile of v2, /device:TPU:17, one launch (start us, length us, event | category | flops | bytes accessed | tf_op | source)
XLA Modules:
  0.0 739.4 jit_solution(4480014451594032208)
XLA Ops:
  0.6 248.3 %forward_save.1 = (bf16[8,4,2,2,2,24,2048]{6,5,4,3,2,1,0:T(8,128)(2,1)}, bf16[8,4,2,2,2,64,768]{6,5,4,3,2,1,0:T(8,128)(2,1)}, f32[1024,768]{1,0:T(8,128)}, f32[8...) custom-call(f32[8,24,2048]{2,1,0:T(8,128)} %refs_0_.1, f32[8,64,768]{2,1,0:T(8,128)} %refs_1_.1, ...), custom_call_target="tpu_custom_call" | custom-call | tf_op jit(solution)/shard_map/forward_save/pallas_call | solution.py:354
  248.9 241.8 %backward.1 = (bf16[8,24,2048]{2,1,0:T(8,128)(2,1)}, bf16[8,64,768]{2,1,0:T(8,128)(2,1)}) custom-call(bf16[8,4,2,2,2,24,2048]{6,5,4,3,2,1,0:T(8,128)(2,1)} %get-tuple-element.15.refs_0_, bf16[8,4,2,2,2,64,768]{6,5,4,3,2,1,0:T(8,128)(2,1)} %get-tuple-element.16.refs_1_, f32[8,1024,2048]{2,1,0:T(8,128)} %get-tuple-element.17.refs_2_, ...), custom_call_target="tpu_custom_call" | custom-call | tf_op jit(solution)/shard_map/backward/pallas_call | solution.py:623
  490.7 0.0 copy-start.1
  490.7 0.0 copy-start.2
  490.7 0.0 copy-start.3
  490.7 4.5 multiply_subtract_fusion.1
  495.3 0.0 copy-done.1
  495.3 0.0 copy-done.2
  495.3 0.0 copy-done.3
  495.3 2.0 multiply_subtract_fusion
  497.3 236.8 %forward_last.1 = (bf16[8,4,2,2,2,24,2048]{6,5,4,3,2,1,0:T(8,128)(2,1)}, bf16[8,4,2,2,2,64,768]{6,5,4,3,2,1,0:T(8,128)(2,1)}, f32[1024,768]{1,0:T(8,128)}) custom-call(f32[8,24,2048]{2,1,0:T(8,128)} %get-tuple-element.34.refs_0_, f32[8,64,768]{2,1,0:T(8,128)} %get-tuple-element.35.refs_1_, bf16[1024,768]{1,0:T(8,128)(2,1)} %refs_2_.3), custom_call_target="tpu_custom_call" | custom-call | tf_op jit(solution)/shard_map/forward_last/pallas_call | solution.py:354
  734.1 0.0 copy-start
  734.1 3.0 multiply_reduce_fusion
  737.1 0.6 broadcast_multiply_fusion
  737.7 0.0 copy-done
  737.7 1.7 copy.15
Async XLA Ops:
  490.7 4.6 copy-start.1
  490.7 4.6 copy-start.2
  490.7 4.6 copy-start.3
  734.1 3.6 copy-start

commit v3 on v2

--- a/solution.py
+++ b/solution.py
@@ -207,18 +207,20 @@
     def zt_save(l):
         return pltpu.make_async_copy(zt_v, zt_out.at[l], save_sem.at[tiles + 1])
 
+    def load(t, l, n):
+        core = 1 - c if n else c
+        return pltpu.make_async_copy(
+            full[t].at[l, :, :, :, core], (w1v, w2v)[t].at[:, :, :, core], load_sem.at[t, n]
+        )
+
     def compute(l):
-        load1 = pltpu.make_async_copy(g1.at[l], w1v, load_sem.at[0])
-        load2 = pltpu.make_async_copy(g2.at[l], w2v, load_sem.at[1])
-        load1.start()
-        load2.start()
         if save:
             @pl.when(l > 0)
             def _():
                 at_save(l - 1).wait()
                 zt_save(l - 1).wait()
-        load1.wait()
-        load2.wait()
+        for n in (0, 1):
+            load(0, l, n).wait()
 
         def tile(m, carry):
             start = pl.multiple_of(m * TILE, TILE)
@@ -226,6 +228,12 @@
             a = h[rows, :].astype(BF16)
             u = dot(a, whole(w1v))
             act = gelu(u).astype(BF16)
+
+            @pl.when(m == 0)
+            def _():
+                for n in (0, 1):
+                    load(1, l, n).wait()
+
             if save:
                 @pl.when(l > 0)
                 def _():
@@ -254,6 +262,9 @@
         to_core(t, 0)
 
     def step(l, carry):
+        for t in (0, 1):
+            load(t, l, 0).start()
+
         @pl.when(l + AHEAD < layers)
         def _():
             send_z(l + AHEAD, 0)
@@ -281,6 +292,7 @@
         for t in (0, 1):
             hop(t, 2, l, True).wait_recv()
             hop(t, 3, l, True).wait_recv()
+            load(t, l, 1).start()
         compute(l)
 
         @pl.when(l + 1 < layers)
@@ -337,7 +349,7 @@
         pltpu.VMEM((4, 2, 2, 2, r1, d_ff), BF16),
         pltpu.VMEM((4, 2, 2, 2, r2, d_model), BF16),
         pltpu.SemaphoreType.DMA((2,)),
-        pltpu.SemaphoreType.DMA((2,)),
+        pltpu.SemaphoreType.DMA((2, 2)),
         pltpu.SemaphoreType.DMA((2, 9)),
         pltpu.SemaphoreType.DMA((2, layers, 8)),
         pltpu.SemaphoreType.DMA((2, 2, 6)),

time: 740 us -> 734 us (level)
  no operation moved by 1% of the time
where the time goes in v3:
time: 734 us
  Pallas kernels  721 us (98%)
  other arithmetic  10.2 us (1%)
    pallas_call x2, Pallas kernels, forward(): pl.pallas_call(functools.partial(forward_kernel, save, scale), out_shape=...  481 us
    pallas_call x1, Pallas kernels, backward(): pl.pallas_call(backward_kernel, out_shape=[sds((layers, r1, d_ff), BF16),...  241 us

profile of v3, /device:TPU:17, one launch (start us, length us, event | category | flops | bytes accessed | tf_op | source)
XLA Modules:
  0.0 733.9 jit_solution(14149412810750573442)
XLA Ops:
  0.6 242.0 %forward_save.1 = (bf16[8,4,2,2,2,24,2048]{6,5,4,3,2,1,0:T(8,128)(2,1)}, bf16[8,4,2,2,2,64,768]{6,5,4,3,2,1,0:T(8,128)(2,1)}, f32[1024,768]{1,0:T(8,128)}, f32[8...) custom-call(f32[8,24,2048]{2,1,0:T(8,128)} %refs_0_.1, f32[8,64,768]{2,1,0:T(8,128)} %refs_1_.1, ...), custom_call_target="tpu_custom_call" | custom-call | tf_op jit(solution)/shard_map/forward_save/pallas_call | solution.py:366
  242.7 240.5 %backward.1 = (bf16[8,24,2048]{2,1,0:T(8,128)(2,1)}, bf16[8,64,768]{2,1,0:T(8,128)(2,1)}) custom-call(bf16[8,4,2,2,2,24,2048]{6,5,4,3,2,1,0:T(8,128)(2,1)} %get-tuple-element.15.refs_0_, bf16[8,4,2,2,2,64,768]{6,5,4,3,2,1,0:T(8,128)(2,1)} %get-tuple-element.16.refs_1_, f32[8,1024,2048]{2,1,0:T(8,128)} %get-tuple-element.17.refs_2_, ...), custom_call_target="tpu_custom_call" | custom-call | tf_op jit(solution)/shard_map/backward/pallas_call | solution.py:635
  483.2 0.0 copy-start.1
  483.2 0.0 copy-start.2
  483.2 0.0 copy-start.3
  483.2 4.5 multiply_subtract_fusion.1
  487.8 0.0 copy-done.1
  487.8 0.0 copy-done.2
  487.8 0.0 copy-done.3
  487.8 2.0 multiply_subtract_fusion
  489.8 238.9 %forward_last.1 = (bf16[8,4,2,2,2,24,2048]{6,5,4,3,2,1,0:T(8,128)(2,1)}, bf16[8,4,2,2,2,64,768]{6,5,4,3,2,1,0:T(8,128)(2,1)}, f32[1024,768]{1,0:T(8,128)}) custom-call(f32[8,24,2048]{2,1,0:T(8,128)} %get-tuple-element.34.refs_0_, f32[8,64,768]{2,1,0:T(8,128)} %get-tuple-element.35.refs_1_, bf16[1024,768]{1,0:T(8,128)(2,1)} %refs_2_.3), custom_call_target="tpu_custom_call" | custom-call | tf_op jit(solution)/shard_map/forward_last/pallas_call | solution.py:366
  728.7 0.0 copy-start
  728.7 3.0 multiply_reduce_fusion
  731.7 0.6 broadcast_multiply_fusion
  732.3 0.0 copy-done
  732.3 1.7 copy.15
Async XLA Ops:
  483.2 4.6 copy-start.1
  483.2 4.6 copy-start.2
  483.2 4.6 copy-start.3
  728.7 3.6 copy-start
